TPU v7x, 32 devices: a whole 2x2x4 slice. The times are simulated.
32 devices in a mesh: occ: 8 (over y, x, core), frag: 4 (over z).
Axes of the slice: x: 2, y: 2, z: 4, core: 2. Of those that a mesh axis runs over, the one named last changes fastest.
Arguments:
- factors: bfloat16 [32, 512, 1280], P(('frag', 'occ')), parts along dimension 0, may hold values from -1 to 1
- occ_energy: float32 [32], P('frag'), parts along dimension 0, may hold values from -2 to -0.3
- vir_energy: float32 [2048], P('frag'), parts along dimension 0, may hold values from 0.2 to 4
- coeffs: bfloat16 [4096, 512], P('frag'), parts along dimension 0, may hold values from -0.25 to 0.25
Outputs:
- back: bfloat16 [1280, 32, 1024], P('occ', 'frag'), parts along dimension 1
There are 4 independent parts, one for each index of `frag`. A program takes and returns all parts, laid end to end along the dimension named above; each array names one. Nothing has to cross between parts.
All inputs are finite; a program needn't handle non-finite values.
Results may differ from a plain program's by a relative error of at most 0.008.
Values may be sent and summed in bfloat16 or wider, within the bound.
A program may use at most 64 MiB of HBM per device.

v0:
```python
import jax
import jax.numpy as jnp
from jax import lax
from jax.sharding import PartitionSpec as P

OFFSETS = 3


def passed_along(block, axis, distance):
    devices = range(lax.axis_size(axis))
    route = [((i - distance) % len(devices), i) for i in devices]
    return lax.ppermute(block, axis, route)


def on_device(factors, occ_energy, vir_energy, coeffs):
    mine = factors[0]
    count = lax.axis_size("occ")
    index = lax.axis_index("occ")
    partners = []
    current = mine
    for offset in range(1, OFFSETS + 1):
        current = passed_along(current, "occ", -1)
        partners.append(current)
    own_energy = lax.dynamic_index_in_dim(occ_energy, index, 0, False)
    own = jnp.zeros((mine.shape[1], mine.shape[0]), jnp.float32)
    outgoing = []
    for offset in range(1, OFFSETS + 1):
        partner = partners[offset - 1]
        other_energy = lax.dynamic_index_in_dim(occ_energy, (index + offset) % count, 0, False)
        kmat = lax.dot_general(
            mine, partner, (((1,), (1,)), ((), ())), preferred_element_type=jnp.float32
        )
        denom = own_energy + other_energy - vir_energy[:, None] - vir_energy[None, :]
        amps = (kmat / denom).astype(jnp.bfloat16)
        own = own + lax.dot_general(
            partner, amps, (((0,), (1,)), ((), ())), preferred_element_type=jnp.float32
        )
        sent = lax.dot_general(
            mine, amps, (((0,), (0,)), ((), ())), preferred_element_type=jnp.float32
        )
        outgoing.append(sent.astype(jnp.bfloat16))
    incoming = jnp.zeros_like(own)
    for offset in range(1, OFFSETS + 1):
        arrived = passed_along(outgoing[offset - 1], "occ", offset)
        incoming = incoming + arrived.astype(jnp.float32)
    gamma = (own + incoming).astype(jnp.bfloat16)[None]
    slabs = lax.all_to_all(gamma, "occ", split_axis=1, concat_axis=0, tiled=True)
    return jnp.einsum("ipa,ma->pim", slabs, coeffs, preferred_element_type=jnp.float32).astype(
        jnp.bfloat16
    )


def solution(mesh):
    return jax.shard_map(
        on_device,
        mesh=mesh,
        in_specs=(P(("frag", "occ"), None, None), P("frag"), P("frag"), P("frag", None)),
        out_specs=P("occ", "frag", None),
        check_vma=False,
    )
```

profile of v0, /device:TPU:0, one launch (start us, length us, event | category | flops | bytes accessed | tf_op | source)
XLA Modules:
  0.0 173.1 jit_solution(9468343890820798394)
XLA Ops:
  0.0 3.4 %collective-permute-start = (bf16[512,1280]{1,0:T(8,128)(2,1)}, bf16[512,1280]{1,0:T(8,128)(2,1)}, u32[]{:S(2)}, u32[]{:S(2)}) collective-permute-start(bf16[512,1280]{1,0:T(8,128)(2,1)} %bitcast.56), channel_id=1, source_target_pairs={{4,0},{8,4},{12,8},{16,12},{20,16},{24,20},{28,24},{0,28},{5,1},{9... | collective-permute-start | bytes 3932168 | tf_op jit(solution)/shard_map/ppermute | solution.py:12
  3.4 15.4 %collective-permute-done = bf16[512,1280]{1,0:T(8,128)(2,1)} collective-permute-done((bf16[512,1280]{1,0:T(8,128)(2,1)}, bf16[512,1280]{1,0:T(8,128)(2,1)}, u32[]{:S(2)}, u32[]{:S(2)}) %collective-permute-start) | collective-permute-done | bytes 1310752 | tf_op jit(solution)/shard_map/ppermute | solution.py:12
  18.8 2.8 %collective-permute-start.1 = (bf16[512,1280]{1,0:T(8,128)(2,1)}, bf16[512,1280]{1,0:T(8,128)(2,1)S(1)}, u32[]{:S(2)}, u32[]{:S(2)}) collective-permute-start(bf16[512,1280]{1,0:T(8,128)(2,1)} %collective-permute-done), channel_id=1, source_target_pairs={{4,0},{8,4},{12,8},{16,12},{20,16},{24,20},{28,24},{0,28},{5,1},{9... | collective-permute-start | bytes 3932168 | tf_op jit(solution)/shard_map/ppermute | solution.py:12
  21.6 1.5 fusion.17
  27.5 9.5 %collective-permute-done.1 = bf16[512,1280]{1,0:T(8,128)(2,1)S(1)} collective-permute-done((bf16[512,1280]{1,0:T(8,128)(2,1)}, bf16[512,1280]{1,0:T(8,128)(2,1)S(1)}, u32[]{:S(2)}, u32[]{:S(2)}) %collective-permute-start.1) | collective-permute-done | bytes 1310752 | tf_op jit(solution)/shard_map/ppermute | solution.py:12
  37.1 2.7 %collective-permute-start.2 = (bf16[512,1280]{1,0:T(8,128)(2,1)S(1)}, bf16[512,1280]{1,0:T(8,128)(2,1)S(1)}, u32[]{:S(2)}, u32[]{:S(2)}) collective-permute-start(bf16[512,1280]{1,0:T(8,128)(2,1)S(1)} %collective-permute-done.1), channel_id=1, source_target_pairs={{4,0},{8,4},{12,8},{16,12},{20,16},{24,20},{28,24},{0,28},{5,1},{9... | collective-permute-start | bytes 3932168 | tf_op jit(solution)/shard_map/ppermute | solution.py:12
  39.8 2.7 %fusion.7 = bf16[512,512]{1,0:T(8,128)(2,1)S(1)} fusion(bf16[512,1280]{1,0:T(8,128)(2,1)} %collective-permute-done, f32[512]{0:T(512)} %param.6, f32[512]{0:T(512)S(1)} %get-tuple-element.6, bf16[1,512,1280]{2,1,0:T(8,128)(2,1)} %param.4), kind=kOutput, calls=%fused_computation.16 | convolution fusion | flops 671875072 | bytes 3149824 | tf_op jit(solution)/shard_map/dot_general | solution.py:30
  43.4 0.9 fusion.8
  45.3 22.8 %collective-permute-done.2 = bf16[512,1280]{1,0:T(8,128)(2,1)S(1)} collective-permute-done((bf16[512,1280]{1,0:T(8,128)(2,1)S(1)}, bf16[512,1280]{1,0:T(8,128)(2,1)S(1)}, u32[]{:S(2)}, u32[]{:S(2)}) %collective-permute-start.2) | collective-permute-done | bytes 1310752 | tf_op jit(solution)/shard_map/ppermute | solution.py:12
  68.0 0.9 fusion.9
  69.8 0.9 collective-permute-start.5
  70.7 2.2 %fusion.18 = f32[512,1280]{1,0:T(8,128)S(1)} fusion(bf16[512,512]{1,0:T(8,128)(2,1)S(1)} %fusion.7, bf16[512,1280]{1,0:T(8,128)(2,1)} %collective-permute-done), kind=kOutput, calls=%fused_computation.30 | convolution fusion | flops 671088640 | bytes 4456448 | tf_op jit(solution)/shard_map/dot_general | solution.py:35
  73.7 1.8 %collective-permute-done.3 = bf16[1280,512]{0,1:T(8,128)(2,1)S(1)} collective-permute-done((bf16[1280,512]{0,1:T(8,128)(2,1)S(1)}, bf16[1280,512]{0,1:T(8,128)(2,1)S(1)}, u32[]{:S(2)}, u32[]{:S(2)}) %collective-permute-start.3) | collective-permute-done | bytes 1310752 | tf_op jit(solution)/shard_map/ppermute | solution.py:12
  75.5 20.6 %collective-permute-done.4 = bf16[1280,512]{0,1:T(8,128)(2,1)S(1)} collective-permute-done((bf16[1280,512]{0,1:T(8,128)(2,1)S(1)}, bf16[1280,512]{0,1:T(8,128)(2,1)S(1)}, u32[]{:S(2)}, u32[]{:S(2)}) %collective-permute-start.4) | collective-permute-done | bytes 1310752 | tf_op jit(solution)/shard_map/ppermute | solution.py:12
  96.1 28.2 %collective-permute-done.5 = bf16[1280,512]{0,1:T(8,128)(2,1)S(1)} collective-permute-done((bf16[1280,512]{0,1:T(8,128)(2,1)S(1)}, bf16[1280,512]{0,1:T(8,128)(2,1)S(1)}, u32[]{:S(2)}, u32[]{:S(2)}) %collective-permute-start.5) | collective-permute-done | bytes 1310752 | tf_op jit(solution)/shard_map/ppermute | solution.py:12
  124.3 0.9 fusion.6
  125.3 4.1 %copy.9 = bf16[1,1280,512]{2,0,1:T(2,128)(2,1)} copy(bf16[1,1280,512]{1,2,0:T(8,128)(2,1)S(1)} %fusion.6) | data formatting | bytes 2621440 | tf_op jit(solution)/shard_map/broadcast_in_dim | solution.py:46
  129.9 9.5 %reduce = bf16[1280,512]{1,0:T(8,128)(2,1)S(1)} reduce(bf16[1280,1,512]{2,1,0:T(2,128)(2,1)} %bitcast.53, bf16[]{:T(256)} %broadcast.10), dimensions={1}, to_apply=%bitcast.38.reduce_sub_computation | reduce | bytes 2621442
  139.4 1.8 %reshape.14 = bf16[8,2,40960]{2,1,0:T(2,128)(2,1)} reshape(bf16[1280,512]{1,0:T(8,128)(2,1)S(1)} %reduce) | data formatting | bytes 2621440
  141.2 21.6 %all_to_all.12 = bf16[8,2,40960]{2,1,0:T(2,128)(2,1)S(1)} all-to-all(bf16[8,2,40960]{2,1,0:T(2,128)(2,1)} %reshape.14), channel_id=1, replica_groups=mesh['occ'=8,'frag'=4] {'occ'}, dimensions={0} | all-to-all | bytes 2621440 | tf_op jit(solution)/shard_map/all_to_all | solution.py:47
  162.8 3.6 %reshape.15 = bf16[1280,1,512]{2,1,0:T(2,128)(2,1)} reshape(bf16[8,2,40960]{2,1,0:T(2,128)(2,1)S(1)} %all_to_all.12) | data formatting | bytes 2621440
  166.5 2.1 %copy.11 = bf16[1,1280,512]{2,1,0:T(8,128)(2,1)S(1)} copy(bf16[1,1280,512]{2,0,1:T(2,128)(2,1)} %bitcast.54) | data formatting | bytes 2621440
  168.6 1.6 convert_bitcast_fusion
  170.2 2.9 %copy.10 = bf16[160,8,1024]{2,1,0:T(8,128)(2,1)} copy(bf16[160,8,1024]{2,0,1:T(8,128)(2,1)S(1)} %convert_bitcast_fusion) | data formatting | bytes 5242880 | tf_op jit(solution)/shard_map/convert_element_type | solution.py:48
  (14 shorter events, 4.9 us)
Async XLA Ops:
  0.0 168.6 %copy-start = (bf16[1024,512]{1,0:T(8,128)(2,1)S(1)}, bf16[1024,512]{1,0:T(8,128)(2,1)}, u32[]{:S(2)}) copy-start(bf16[1024,512]{1,0:T(8,128)(2,1)} %param.7) | copy-start | bytes 3145732
  0.0 18.8 %collective-permute-start = (bf16[512,1280]{1,0:T(8,128)(2,1)}, bf16[512,1280]{1,0:T(8,128)(2,1)}, u32[]{:S(2)}, u32[]{:S(2)}) collective-permute-start(bf16[512,1280]{1,0:T(8,128)(2,1)} %bitcast.56), channel_id=1, source_target_pairs={{4,0},{8,4},{12,8},{16,12},{20,16},{24,20},{28,24},{0,28},{5,1},{9... | collective-permute-start | bytes 3932168 | tf_op jit(solution)/shard_map/ppermute | solution.py:12
  18.8 18.2 %collective-permute-start.1 = (bf16[512,1280]{1,0:T(8,128)(2,1)}, bf16[512,1280]{1,0:T(8,128)(2,1)S(1)}, u32[]{:S(2)}, u32[]{:S(2)}) collective-permute-start(bf16[512,1280]{1,0:T(8,128)(2,1)} %collective-permute-done), channel_id=1, source_target_pairs={{4,0},{8,4},{12,8},{16,12},{20,16},{24,20},{28,24},{0,28},{5,1},{9... | collective-permute-start | bytes 3932168 | tf_op jit(solution)/shard_map/ppermute | solution.py:12
  37.1 31.0 %collective-permute-start.2 = (bf16[512,1280]{1,0:T(8,128)(2,1)S(1)}, bf16[512,1280]{1,0:T(8,128)(2,1)S(1)}, u32[]{:S(2)}, u32[]{:S(2)}) collective-permute-start(bf16[512,1280]{1,0:T(8,128)(2,1)S(1)} %collective-permute-done.1), channel_id=1, source_target_pairs={{4,0},{8,4},{12,8},{16,12},{20,16},{24,20},{28,24},{0,28},{5,1},{9... | collective-permute-start | bytes 3932168 | tf_op jit(solution)/shard_map/ppermute | solution.py:12
  39.8 2.7 %copy-start.2 = (bf16[1,512,1280]{2,1,0:T(8,128)(2,1)S(1)}, bf16[1,512,1280]{2,1,0:T(8,128)(2,1)}, u32[]{:S(2)}) copy-start(bf16[1,512,1280]{2,1,0:T(8,128)(2,1)} %param.4) | copy-start | bytes 3932164
  42.5 1.0 copy-start.1
  43.4 32.1 %collective-permute-start.3 = (bf16[1280,512]{0,1:T(8,128)(2,1)S(1)}, bf16[1280,512]{0,1:T(8,128)(2,1)S(1)}, u32[]{:S(2)}, u32[]{:S(2)}) collective-permute-start(bf16[1280,512]{0,1:T(8,128)(2,1)S(1)} %fusion.3), channel_id=1, source_target_pairs={{28,0},{0,4},{4,8},{8,12},{12,16},{16,20},{20,24},{24,28},{29,1},{... | collective-permute-start | bytes 3932168 | tf_op jit(solution)/shard_map/ppermute | solution.py:12
  45.2 50.9 %collective-permute-start.4 = (bf16[1280,512]{0,1:T(8,128)(2,1)S(1)}, bf16[1280,512]{0,1:T(8,128)(2,1)S(1)}, u32[]{:S(2)}, u32[]{:S(2)}) collective-permute-start(bf16[1280,512]{0,1:T(8,128)(2,1)S(1)} %fusion.4), channel_id=1, source_target_pairs={{24,0},{28,4},{0,8},{4,12},{8,16},{12,20},{16,24},{20,28},{25,1},{... | collective-permute-start | bytes 3932168 | tf_op jit(solution)/shard_map/ppermute | solution.py:12
  69.8 54.5 %collective-permute-start.5 = (bf16[1280,512]{0,1:T(8,128)(2,1)S(1)}, bf16[1280,512]{0,1:T(8,128)(2,1)S(1)}, u32[]{:S(2)}, u32[]{:S(2)}) collective-permute-start(bf16[1280,512]{0,1:T(8,128)(2,1)S(1)} %fusion.5), channel_id=1, source_target_pairs={{20,0},{24,4},{28,8},{0,12},{4,16},{8,20},{12,24},{16,28},{21,1},{... | collective-permute-start | bytes 3932168 | tf_op jit(solution)/shard_map/ppermute | solution.py:12
where the time goes:
time: 173 us
  waiting for transfers between devices  98.4 us (57%)
  blocking collectives  21.6 us (12%)
  local copies, waits for them, and re-layouts  16.6 us (10%)
  matrix products  12.6 us (7%)
  other arithmetic  10.2 us (6%)
  starting transfers between devices  9.87 us (6%)
  between operations  3.89 us (2%)
    ppermute x6, waiting for transfers between devices, passed_along(): return lax.ppermute(block, axis, route)  98.4 us
    all_to_all x1, blocking collectives, on_device(): lax.all_to_all(gamma, 'occ', split_axis=1, concat_axis=0, tiled=True)  21.6 us
    ppermute x6, starting transfers between devices, passed_along(): return lax.ppermute(block, axis, route)  9.87 us
    unnamed x1, other arithmetic  9.47 us
    unnamed x10, local copies, waits for them, and re-layouts  8.17 us
    dot_general x3, matrix products, on_device(): lax.dot_general(mine, partner, (((1,), (1,)), ((), ())), preferred_elemen...  4.45 us
    broadcast_in_dim x1, local copies, waits for them, and re-layouts, on_device(): gamma = (own + incoming).astype(jnp.bfloat16)[None]  4.07 us
    dot_general x3, matrix products, on_device(): lax.dot_general(partner, amps, (((0,), (1,)), ((), ())), preferred_elemen...  3.94 us
  transfers between devices with their start and end apart: 6, of which 6 were waited for; matrix products, arithmetic and copies ran while one was open for 7% of the time, Pallas kernels for 0%

commit v1 on v0

--- a/solution.py
+++ b/solution.py
@@ -1,9 +1,19 @@
+import functools
 import jax
 import jax.numpy as jnp
 from jax import lax
 from jax.sharding import PartitionSpec as P
 
 OFFSETS = 3
+
+
+def list_types(field, peer_axis):
+    return jnp.concatenate(
+        lax.all_to_all(jnp.stack(jnp.split(field, lax.axis_size(peer_axis), 1)), peer_axis, 0, 0), 0
+    )
+
+
+follow_the_streams = functools.partial(list_types, peer_axis="occ")
 
 
 def passed_along(block, axis, distance):
@@ -44,7 +54,7 @@
         arrived = passed_along(outgoing[offset - 1], "occ", offset)
         incoming = incoming + arrived.astype(jnp.float32)
     gamma = (own + incoming).astype(jnp.bfloat16)[None]
-    slabs = lax.all_to_all(gamma, "occ", split_axis=1, concat_axis=0, tiled=True)
+    slabs = follow_the_streams(gamma)
     return jnp.einsum("ipa,ma->pim", slabs, coeffs, preferred_element_type=jnp.float32).astype(
         jnp.bfloat16
     )

time: 173 us -> 160 us (0.925)
  other arithmetic: 10.2 us -> 0.69 us
  local copies, waits for them, and re-layouts: 16.6 us -> 13.8 us
    unnamed x1 -> x0, other arithmetic: 9.47 us -> none
    broadcast_in_dim x1 -> x0, local copies, waits for them, and re-layouts: 4.07 us -> none  [on_device(): gamma = (own + incoming).astype(jnp.bfloat16)[None]]
    another operation x0 -> x2, local copies, waits for them, and re-layouts: none -> 3.79 us  [list_types(): jnp.stack(jnp.split(field, lax.axis_size(peer_axis), 1))]
    unnamed x10 -> x13, local copies, waits for them, and re-layouts: 8.17 us -> 5.67 us
  transfers between devices with their start and end apart: 6 -> 6, of which waited for: 6 -> 6; matrix products, arithmetic and copies ran while one was open for 7% -> 8% of each run, Pallas kernels for 0% -> 0%
where the time goes in v1:
time: 160 us
  waiting for transfers between devices  98.4 us (62%)
  blocking collectives  20.6 us (13%)
  local copies, waits for them, and re-layouts  13.8 us (9%)
  matrix products  12.6 us (8%)
  starting transfers between devices  9.87 us (6%)
  between operations  3.81 us (2%)
    ppermute x6, waiting for transfers between devices, passed_along(): return lax.ppermute(block, axis, route)  98.4 us
    all_to_all x1, blocking collectives, list_types(): lax.all_to_all(jnp.stack(jnp.split(field, lax.axis_size(peer_axis), 1)),...  20.6 us
    ppermute x6, starting transfers between devices, passed_along(): return lax.ppermute(block, axis, route)  9.87 us
    unnamed x13, local copies, waits for them, and re-layouts  5.67 us
    dot_general x3, matrix products, on_device(): lax.dot_general(mine, partner, (((1,), (1,)), ((), ())), preferred_elemen...  4.45 us
    dot_general x3, matrix products, on_device(): lax.dot_general(partner, amps, (((0,), (1,)), ((), ())), preferred_elemen...  3.94 us
    another operation x2, local copies, waits for them, and re-layouts, list_types(): jnp.stack(jnp.split(field, lax.axis_size(peer_axis), 1))  3.79 us
  transfers between devices with their start and end apart: 6, of which 6 were waited for; matrix products, arithmetic and copies ran while one was open for 8% of the time, Pallas kernels for 0%

profile of v1, /device:TPU:0, one launch (start us, length us, event | category | flops | bytes accessed | tf_op | source)
XLA Modules:
  0.0 159.8 jit_solution(658077072128021899)
XLA Ops:
  0.0 3.4 %collective-permute-start = (bf16[512,1280]{1,0:T(8,128)(2,1)}, bf16[512,1280]{1,0:T(8,128)(2,1)}, u32[]{:S(2)}, u32[]{:S(2)}) collective-permute-start(bf16[512,1280]{1,0:T(8,128)(2,1)} %bitcast.84), channel_id=1, source_target_pairs={{4,0},{8,4},{12,8},{16,12},{20,16},{24,20},{28,24},{0,28},{5,1},{9... | collective-permute-start | bytes 3932168 | tf_op jit(solution)/shard_map/ppermute | solution.py:22
  3.4 15.4 %collective-permute-done = bf16[512,1280]{1,0:T(8,128)(2,1)} collective-permute-done((bf16[512,1280]{1,0:T(8,128)(2,1)}, bf16[512,1280]{1,0:T(8,128)(2,1)}, u32[]{:S(2)}, u32[]{:S(2)}) %collective-permute-start) | collective-permute-done | bytes 1310752 | tf_op jit(solution)/shard_map/ppermute | solution.py:22
  18.8 2.8 %collective-permute-start.1 = (bf16[512,1280]{1,0:T(8,128)(2,1)}, bf16[512,1280]{1,0:T(8,128)(2,1)S(1)}, u32[]{:S(2)}, u32[]{:S(2)}) collective-permute-start(bf16[512,1280]{1,0:T(8,128)(2,1)} %collective-permute-done), channel_id=1, source_target_pairs={{4,0},{8,4},{12,8},{16,12},{20,16},{24,20},{28,24},{0,28},{5,1},{9... | collective-permute-start | bytes 3932168 | tf_op jit(solution)/shard_map/ppermute | solution.py:22
  21.6 1.5 fusion.26
  27.5 9.6 %collective-permute-done.1 = bf16[512,1280]{1,0:T(8,128)(2,1)S(1)} collective-permute-done((bf16[512,1280]{1,0:T(8,128)(2,1)}, bf16[512,1280]{1,0:T(8,128)(2,1)S(1)}, u32[]{:S(2)}, u32[]{:S(2)}) %collective-permute-start.1) | collective-permute-done | bytes 1310752 | tf_op jit(solution)/shard_map/ppermute | solution.py:22
  37.1 2.7 %collective-permute-start.2 = (bf16[512,1280]{1,0:T(8,128)(2,1)S(1)}, bf16[512,1280]{1,0:T(8,128)(2,1)S(1)}, u32[]{:S(2)}, u32[]{:S(2)}) collective-permute-start(bf16[512,1280]{1,0:T(8,128)(2,1)S(1)} %collective-permute-done.1), channel_id=1, source_target_pairs={{4,0},{8,4},{12,8},{16,12},{20,16},{24,20},{28,24},{0,28},{5,1},{9... | collective-permute-start | bytes 3932168 | tf_op jit(solution)/shard_map/ppermute | solution.py:22
  39.8 2.7 %fusion.8 = bf16[512,512]{1,0:T(8,128)(2,1)S(1)} fusion(bf16[512,1280]{1,0:T(8,128)(2,1)} %collective-permute-done, f32[512]{0:T(512)} %param.6, f32[512]{0:T(512)S(1)} %get-tuple-element.6, bf16[1,512,1280]{2,1,0:T(8,128)(2,1)} %param.4), kind=kOutput, calls=%fused_computation.17 | convolution fusion | flops 671875072 | bytes 3149824 | tf_op jit(solution)/shard_map/dot_general | solution.py:40
  42.5 0.9 fusion.3
  43.4 0.9 fusion.9
  44.3 0.9 fusion.4
  45.3 22.8 %collective-permute-done.2 = bf16[512,1280]{1,0:T(8,128)(2,1)S(1)} collective-permute-done((bf16[512,1280]{1,0:T(8,128)(2,1)S(1)}, bf16[512,1280]{1,0:T(8,128)(2,1)S(1)}, u32[]{:S(2)}, u32[]{:S(2)}) %collective-permute-start.2) | collective-permute-done | bytes 1310752 | tf_op jit(solution)/shard_map/ppermute | solution.py:22
  68.0 0.9 fusion.10
  68.9 0.9 fusion.5
  69.8 0.9 collective-permute-start.5
  70.7 2.2 %fusion.27 = f32[512,1280]{1,0:T(8,128)S(1)} fusion(bf16[512,512]{1,0:T(8,128)(2,1)S(1)} %fusion.8, bf16[512,1280]{1,0:T(8,128)(2,1)} %collective-permute-done), kind=kOutput, calls=%fused_computation.47 | convolution fusion | flops 671088640 | bytes 4456448 | tf_op jit(solution)/shard_map/dot_general | solution.py:45
  73.7 1.8 %collective-permute-done.3 = bf16[1280,512]{0,1:T(8,128)(2,1)S(1)} collective-permute-done((bf16[1280,512]{0,1:T(8,128)(2,1)S(1)}, bf16[1280,512]{0,1:T(8,128)(2,1)S(1)}, u32[]{:S(2)}, u32[]{:S(2)}) %collective-permute-start.3) | collective-permute-done | bytes 1310752 | tf_op jit(solution)/shard_map/ppermute | solution.py:22
  75.5 20.6 %collective-permute-done.4 = bf16[1280,512]{0,1:T(8,128)(2,1)S(1)} collective-permute-done((bf16[1280,512]{0,1:T(8,128)(2,1)S(1)}, bf16[1280,512]{0,1:T(8,128)(2,1)S(1)}, u32[]{:S(2)}, u32[]{:S(2)}) %collective-permute-start.4) | collective-permute-done | bytes 1310752 | tf_op jit(solution)/shard_map/ppermute | solution.py:22
  96.1 28.2 %collective-permute-done.5 = bf16[1280,512]{0,1:T(8,128)(2,1)S(1)} collective-permute-done((bf16[1280,512]{0,1:T(8,128)(2,1)S(1)}, bf16[1280,512]{0,1:T(8,128)(2,1)S(1)}, u32[]{:S(2)}, u32[]{:S(2)}) %collective-permute-start.5) | collective-permute-done | bytes 1310752 | tf_op jit(solution)/shard_map/ppermute | solution.py:22
  124.3 0.9 fusion.6
  130.9 0.8 fusion.12
  131.8 2.9 %copy.7 = bf16[8,1,160,512]{3,2,1,0:T(8,128)(2,1)S(1)} copy(bf16[8,1,160,512]{2,3,1,0:T(8,128)(2,1)} %fusion.12) | data formatting | bytes 2621440 | tf_op jit(solution)/shard_map/stack | solution.py:12
  134.7 20.6 %all_to_all.5 = bf16[8,1,160,512]{3,2,1,0:T(8,128)(2,1)S(1)} all-to-all(bf16[8,1,160,512]{3,2,1,0:T(8,128)(2,1)S(1)} %copy.7), channel_id=1, replica_groups=mesh['occ'=8,'frag'=4] {'occ'}, dimensions={0} | all-to-all | bytes 2621440 | tf_op jit(solution)/shard_map/all_to_all | solution.py:12
  155.3 1.6 convert_bitcast_fusion
  156.9 2.9 %copy.8 = bf16[160,8,1024]{2,1,0:T(8,128)(2,1)} copy(bf16[160,8,1024]{2,0,1:T(8,128)(2,1)S(1)} %convert_bitcast_fusion) | data formatting | bytes 5242880 | tf_op jit(solution)/shard_map/convert_element_type | solution.py:58
  (17 shorter events, 7.3 us)
Async XLA Ops:
  0.0 155.3 %copy-start = (bf16[1024,512]{1,0:T(8,128)(2,1)S(1)}, bf16[1024,512]{1,0:T(8,128)(2,1)}, u32[]{:S(2)}) copy-start(bf16[1024,512]{1,0:T(8,128)(2,1)} %param.7) | copy-start | bytes 3145732
  0.0 18.8 %collective-permute-start = (bf16[512,1280]{1,0:T(8,128)(2,1)}, bf16[512,1280]{1,0:T(8,128)(2,1)}, u32[]{:S(2)}, u32[]{:S(2)}) collective-permute-start(bf16[512,1280]{1,0:T(8,128)(2,1)} %bitcast.84), channel_id=1, source_target_pairs={{4,0},{8,4},{12,8},{16,12},{20,16},{24,20},{28,24},{0,28},{5,1},{9... | collective-permute-start | bytes 3932168 | tf_op jit(solution)/shard_map/ppermute | solution.py:22
  18.8 18.2 %collective-permute-start.1 = (bf16[512,1280]{1,0:T(8,128)(2,1)}, bf16[512,1280]{1,0:T(8,128)(2,1)S(1)}, u32[]{:S(2)}, u32[]{:S(2)}) collective-permute-start(bf16[512,1280]{1,0:T(8,128)(2,1)} %collective-permute-done), channel_id=1, source_target_pairs={{4,0},{8,4},{12,8},{16,12},{20,16},{24,20},{28,24},{0,28},{5,1},{9... | collective-permute-start | bytes 3932168 | tf_op jit(solution)/shard_map/ppermute | solution.py:22
  37.1 31.0 %collective-permute-start.2 = (bf16[512,1280]{1,0:T(8,128)(2,1)S(1)}, bf16[512,1280]{1,0:T(8,128)(2,1)S(1)}, u32[]{:S(2)}, u32[]{:S(2)}) collective-permute-start(bf16[512,1280]{1,0:T(8,128)(2,1)S(1)} %collective-permute-done.1), channel_id=1, source_target_pairs={{4,0},{8,4},{12,8},{16,12},{20,16},{24,20},{28,24},{0,28},{5,1},{9... | collective-permute-start | bytes 3932168 | tf_op jit(solution)/shard_map/ppermute | solution.py:22
  39.8 2.7 %copy-start.2 = (bf16[1,512,1280]{2,1,0:T(8,128)(2,1)S(1)}, bf16[1,512,1280]{2,1,0:T(8,128)(2,1)}, u32[]{:S(2)}) copy-start(bf16[1,512,1280]{2,1,0:T(8,128)(2,1)} %param.4) | copy-start | bytes 3932164
  42.5 1.0 copy-start.1
  43.4 32.1 %collective-permute-start.3 = (bf16[1280,512]{0,1:T(8,128)(2,1)S(1)}, bf16[1280,512]{0,1:T(8,128)(2,1)S(1)}, u32[]{:S(2)}, u32[]{:S(2)}) collective-permute-start(bf16[1280,512]{0,1:T(8,128)(2,1)S(1)} %fusion.3), channel_id=1, source_target_pairs={{28,0},{0,4},{4,8},{8,12},{12,16},{16,20},{20,24},{24,28},{29,1},{... | collective-permute-start | bytes 3932168 | tf_op jit(solution)/shard_map/ppermute | solution.py:22
  45.2 50.9 %collective-permute-start.4 = (bf16[1280,512]{0,1:T(8,128)(2,1)S(1)}, bf16[1280,512]{0,1:T(8,128)(2,1)S(1)}, u32[]{:S(2)}, u32[]{:S(2)}) collective-permute-start(bf16[1280,512]{0,1:T(8,128)(2,1)S(1)} %fusion.4), channel_id=1, source_target_pairs={{24,0},{28,4},{0,8},{4,12},{8,16},{12,20},{16,24},{20,28},{25,1},{... | collective-permute-start | bytes 3932168 | tf_op jit(solution)/shard_map/ppermute | solution.py:22
  69.8 54.5 %collective-permute-start.5 = (bf16[1280,512]{0,1:T(8,128)(2,1)S(1)}, bf16[1280,512]{0,1:T(8,128)(2,1)S(1)}, u32[]{:S(2)}, u32[]{:S(2)}) collective-permute-start(bf16[1280,512]{0,1:T(8,128)(2,1)S(1)} %fusion.5), channel_id=1, source_target_pairs={{20,0},{24,4},{28,8},{0,12},{4,16},{8,20},{12,24},{16,28},{21,1},{... | collective-permute-start | bytes 3932168 | tf_op jit(solution)/shard_map/ppermute | solution.py:22
